TPU v7x, 32 devices: a whole 2x2x4 slice. The times are simulated.
32 devices in a mesh: blk: 8 (over z, x), tgt: 4 (over y, core).
Axes of the slice: x: 2, y: 2, z: 4, core: 2. Of those that a mesh axis runs over, the one named last changes fastest.
Arguments:
- sources: float32 [8192, 128], P('blk'), may hold values from -0.5 to 0.5, as said below
- targets: float32 [8192, 128], P(('blk', 'tgt')), may hold values from -0.5 to 0.5, as said below
- duals_init: float32 [8192], P(('blk', 'tgt')), may hold values from -1.5 to 1.5
Outputs:
- source_duals: float32 [8192], P('blk')
- target_duals: float32 [8192], P(('blk', 'tgt'))
Inputs may be any that keep to these rules, and one draw needn't show every extreme that they name: `sources`: coordinates of the source points. `targets`: coordinates of the target points.
All inputs are finite; a program needn't handle non-finite values.
Results may differ from a plain program's by a relative error of at most 0.0001.
Values sent between devices are 32-bit elements; how exact they have to be, the bound alone decides.
A program may use at most 64 MiB of HBM per device.

v0:
```python
import jax
import jax.numpy as jnp
from jax import lax
from jax.sharding import PartitionSpec as P

ITERS = 2
EPS = 0.05


def cost_of(left, left_norm, right, right_norm):
    cross = jnp.dot(
        left, right.T, preferred_element_type=jnp.float32, precision=lax.Precision.HIGHEST
    )
    return left_norm[:, None] + right_norm[None, :] - 2.0 * cross


def body(sources, targets, duals_init):
    src_norm = jnp.sum(sources * sources, axis=1)
    rows_here = sources.shape[0]
    cols_here = targets.shape[0]
    total_dst = cols_here * lax.axis_size("blk") * lax.axis_size("tgt")
    total_src = rows_here * lax.axis_size("blk")
    target_pots = duals_init
    source_pots = jnp.zeros_like(src_norm)
    group_rows = lax.all_gather(targets, "blk", axis=0, tiled=True)
    group_norm = jnp.sum(group_rows * group_rows, axis=1)
    cost_tile = cost_of(sources, src_norm, group_rows, group_norm)
    for repeat in range(ITERS):
        group_pots = lax.all_gather(target_pots, "blk", axis=0, tiled=True)
        scores = (group_pots[None, :] - cost_tile) / EPS
        maxima = jnp.max(scores, axis=1)
        totals = jnp.sum(jnp.exp(scores - maxima[:, None]), axis=1)
        highest = lax.pmax(maxima, "tgt")
        totals = lax.psum(totals * jnp.exp(maxima - highest), "tgt")
        maxima = highest
        source_pots = EPS * -jnp.log(jnp.float32(total_dst)) - EPS * (maxima + jnp.log(totals))
        col_scores = (source_pots[:, None] - cost_tile) / EPS
        col_high = lax.pmax(jnp.max(col_scores, axis=0), "blk")
        col_part = jnp.sum(jnp.exp(col_scores - col_high[None, :]), axis=0)
        col_total = lax.psum_scatter(col_part, "blk", scatter_dimension=0, tiled=True)
        own_high = lax.dynamic_slice_in_dim(
            col_high, lax.axis_index("blk") * cols_here, cols_here, 0
        )
        target_pots = EPS * -jnp.log(jnp.float32(total_src)) - EPS * (own_high + jnp.log(col_total))
    return (source_pots, target_pots)


def solution(mesh):
    return jax.shard_map(
        body,
        mesh=mesh,
        in_specs=(P("blk", None), P(("blk", "tgt"), None), P(("blk", "tgt"))),
        out_specs=(P("blk"), P(("blk", "tgt"))),
        check_vma=False,
    )
```

profile of v0, /device:TPU:0, one launch (start us, length us, event | category | flops | bytes accessed | tf_op | source)
XLA Modules:
  0.0 220.8 jit_solution(6186228106651673261)
XLA Ops:
  7.2 0.0 all-gather.4.cloned.1.call-start
  7.2 0.7 all-gather.4.cloned.1.call-update
  7.9 1.2 dynamic-slice
  9.8 22.5 %all-gather = f32[8,1,256]{2,1,0:T(1,128)S(1)} all-gather(f32[1,1,256]{2,1,0:T(1,128)} %bitcast.12), channel_id=1, replica_groups=mesh['blk'=8,'tgt'=4] {'blk'}, dimensions={0}, use_global_device_ids=true | all-gather | bytes 9216 | tf_op jit(solution)/shard_map/all_gather | solution.py:29
  32.3 1.2 multiply_reduce_fusion.1
  33.6 19.5 %all-gather.4.cloned.1.call-done = f32[2048,128]{1,0:T(8,128)} async-done(((f32[256,128]{1,0:T(8,128)}), f32[2048,128]{1,0:T(8,128)}) %all-gather.4.cloned.1.call-update) | async-done | bytes 1048592 | tf_op jit(solution)/shard_map/all_gather | solution.py:25
  53.1 1.6 multiply_reduce_fusion
  54.7 11.5 %fusion = (f32[1024]{0:T(1024)S(1)}, f32[1024,2048]{1,0:T(8,128)}) fusion(f32[2048]{0:T(1024)S(1)} %bitcast.9, f32[1024,128]{1,0:T(8,128)} %param.3, f32[2048,128]{1,0:T(8,128)} %all-gather.4.cloned.1.call-done, f32[2048]{0:T(1024)S(1)} %multiply_reduce_fusion, f32[1024]{0:T(1024)S(1)} %multiply_reduce_fusion.1), kind=kOutput, calls=%fused_computation.9 | convolution fusion | flops 3233807360 | bytes 9986048 | tf_op jit(solution)/shard_map/dot_general | solution.py:11
  66.2 5.6 %pmax.28 = f32[1024]{0:T(1024)S(1)} all-reduce(f32[1024]{0:T(1024)S(1)} %get-tuple-element.2), channel_id=1, replica_groups=mesh['blk'=8,'tgt'=4] {'tgt'}, use_global_device_ids=true, to_apply=%region_3.0 | all-reduce | flops 1024 | bytes 8192 | tf_op jit(solution)/shard_map/pmax | solution.py:33
  71.8 4.5 %exponential_reduce_fusion.3 = f32[1024]{0:T(1024)S(1)} fusion(f32[1024,2048]{1,0:T(8,128)} %get-tuple-element.3, f32[1024]{0:T(1024)S(1)} %get-tuple-element.2, f32[2048]{0:T(1024)S(1)} %bitcast.10), kind=kLoop, calls=%fused_computation.6 | loop fusion | flops 8387584 | bytes 8404992 | tf_op jit(solution)/shard_map/reduce_sum | solution.py:32
  76.4 6.6 %psum.14 = f32[1024]{0:T(1024)S(1)} all-reduce(f32[1024]{0:T(1024)S(1)} %exponential_multiply_fusion.1), channel_id=1, replica_groups=mesh['blk'=8,'tgt'=4] {'tgt'}, use_global_device_ids=true, to_apply=%region_5.0 | all-reduce | flops 1024 | bytes 8192 | tf_op jit(solution)/shard_map/psum | solution.py:34
  83.0 4.3 %fusion.1 = f32[2048]{0:T(1024)S(1)} fusion(f32[1024,2048]{1,0:T(8,128)} %get-tuple-element.3, f32[1024]{0:T(1024)S(1)} %multiply_subtract_fusion.2), kind=kLoop, calls=%fused_computation.10 | loop fusion | flops 6289408 | bytes 8400896 | tf_op jit(solution)/shard_map/reduce_max | solution.py:38
  87.3 19.4 %pmax.29 = f32[2048]{0:T(1024)S(1)} all-reduce(f32[2048]{0:T(1024)S(1)} %fusion.1), channel_id=1, replica_groups=mesh['blk'=8,'tgt'=4] {'blk'}, use_global_device_ids=true, to_apply=%region_7.0 | all-reduce | flops 2048 | bytes 16384 | tf_op jit(solution)/shard_map/pmax | solution.py:38
  106.7 4.5 %exponential_reduce_fusion.2 = f32[2048]{0:T(1024)S(1)} fusion(f32[1024,2048]{1,0:T(8,128)} %get-tuple-element.3, f32[2048]{0:T(1024)S(1)} %pmax.29, f32[1024]{0:T(1024)S(1)} %multiply_subtract_fusion.2), kind=kLoop, calls=%fused_computation.4 | loop fusion | flops 8386560 | bytes 8409088 | tf_op jit(solution)/shard_map/reduce_sum | solution.py:39
  111.2 17.4 %all-reduce = f32[2048]{0:T(1024)S(1)} all-reduce(f32[2048]{0:T(1024)S(1)} %exponential_reduce_fusion.2), channel_id=2, replica_groups=mesh['blk'=8,'tgt'=4] {'blk'}, use_global_device_ids=true, to_apply=%region_9.0.clone | all-reduce | flops 2048 | bytes 16384
  128.6 0.1 fusion.9
  128.7 18.2 %all-gather.1 = f32[8,1,256]{2,1,0:T(1,128)S(1)} all-gather(f32[1,1,256]{2,1,0:T(1,128)S(1)} %bitcast.11), channel_id=1, replica_groups=mesh['blk'=8,'tgt'=4] {'blk'}, dimensions={0}, use_global_device_ids=true | all-gather | bytes 9216 | tf_op jit(solution)/shard_map/all_gather | solution.py:29
  147.0 4.3 %fusion.2 = f32[1024]{0:T(1024)S(1)} fusion(f32[1024,2048]{1,0:T(8,128)} %get-tuple-element.3, f32[2048]{0:T(1024)S(1)} %bitcast.7), kind=kLoop, calls=%fused_computation.11 | loop fusion | flops 6290432 | bytes 8400896 | tf_op jit(solution)/shard_map/reduce_max | solution.py:31
  151.3 4.5 %exponential_reduce_fusion.1 = f32[1024]{0:T(1024)S(1)} fusion(f32[1024,2048]{1,0:T(8,128)} %get-tuple-element.3, f32[1024]{0:T(1024)S(1)} %fusion.2, f32[2048]{0:T(1024)S(1)} %bitcast.8), kind=kLoop, calls=%fused_computation.2 | loop fusion | flops 8387584 | bytes 8404992 | tf_op jit(solution)/shard_map/reduce_sum | solution.py:32
  155.8 5.7 %pmax.30 = f32[1024]{0:T(1024)S(1)} all-reduce(f32[1024]{0:T(1024)S(1)} %fusion.2), channel_id=1, replica_groups=mesh['blk'=8,'tgt'=4] {'tgt'}, use_global_device_ids=true, to_apply=%region_11.0 | all-reduce | flops 1024 | bytes 8192 | tf_op jit(solution)/shard_map/pmax | solution.py:33
  161.5 6.3 %psum.15 = f32[1024]{0:T(1024)S(1)} all-reduce(f32[1024]{0:T(1024)S(1)} %exponential_multiply_fusion), channel_id=1, replica_groups=mesh['blk'=8,'tgt'=4] {'tgt'}, use_global_device_ids=true, to_apply=%region_13.0 | all-reduce | flops 1024 | bytes 8192 | tf_op jit(solution)/shard_map/psum | solution.py:34
  167.7 0.0 copy-start
  167.7 4.3 %fusion.3 = f32[2048]{0:T(1024)S(1)} fusion(f32[1024,2048]{1,0:T(8,128)} %get-tuple-element.3, f32[1024]{0:T(1024)S(1)} %multiply_subtract_fusion.1), kind=kLoop, calls=%fused_computation.12 | loop fusion | flops 6289408 | bytes 8400896 | tf_op jit(solution)/shard_map/reduce_max | solution.py:38
  172.0 17.4 %pmax.31 = f32[2048]{0:T(1024)S(1)} all-reduce(f32[2048]{0:T(1024)S(1)} %fusion.3), channel_id=1, replica_groups=mesh['blk'=8,'tgt'=4] {'blk'}, use_global_device_ids=true, to_apply=%region_15.0 | all-reduce | flops 2048 | bytes 16384 | tf_op jit(solution)/shard_map/pmax | solution.py:38
  189.4 4.5 %exponential_reduce_fusion = f32[2048]{0:T(1024)S(1)} fusion(f32[1024,2048]{1,0:T(8,128)} %get-tuple-element.3, f32[2048]{0:T(1024)S(1)} %pmax.31, f32[1024]{0:T(1024)S(1)} %multiply_subtract_fusion.1), kind=kLoop, calls=%fused_computation | loop fusion | flops 8386560 | bytes 8409088 | tf_op jit(solution)/shard_map/reduce_sum | solution.py:39
  193.9 0.0 copy-done
  193.9 19.4 %all-reduce.1 = f32[2048]{0:T(1024)S(1)} all-reduce(f32[2048]{0:T(1024)S(1)} %exponential_reduce_fusion), channel_id=3, replica_groups=mesh['blk'=8,'tgt'=4] {'blk'}, use_global_device_ids=true, to_apply=%region_17.0.clone | all-reduce | flops 2048 | bytes 16384
  213.3 0.7 fusion.6
  (4 shorter events, 0.0 us)
Async XLA Ops:
  7.2 46.0 %all-gather.4.cloned.1.call-start = ((), (), s32[]{:S(2)}) async-start(), calls=%async_computation | async-start | bytes 1179648 | tf_op jit(solution)/shard_map/all_gather | solution.py:25
  167.7 26.2 %copy-start = (f32[1024]{0:T(1024)}, f32[1024]{0:T(1024)S(1)}, u32[]{:S(2)}) copy-start(f32[1024]{0:T(1024)S(1)} %multiply_subtract_fusion.1) | copy-start | bytes 12292
Sparse Core Ops, SparseCore 0:
  10.1 42.9 all-gather.3
where the time goes:
time: 221 us
  blocking collectives  139 us (63%)
  other arithmetic  34.5 us (16%)
  waiting for transfers between devices  20.2 us (9%)
  between operations  14.8 us (7%)
  matrix products  11.5 us (5%)
    all_gather x2, blocking collectives, body(): group_pots = lax.all_gather(target_pots, 'blk', axis=0, tiled=True)  40.8 us
    unnamed x2, blocking collectives  36.8 us
    pmax x2, blocking collectives, body(): col_high = lax.pmax(jnp.max(col_scores, axis=0), 'blk')  36.8 us
    all_gather x1, waiting for transfers between devices, body(): group_rows = lax.all_gather(targets, 'blk', axis=0, tiled=True)  19.5 us
    psum x2, blocking collectives, body(): totals = lax.psum(totals * jnp.exp(maxima - highest), 'tgt')  12.9 us
    dot_general x1, matrix products, cost_of(): jnp.dot(left, right.T, preferred_element_type=jnp.float32, precision=lax....  11.5 us
    pmax x2, blocking collectives, body(): highest = lax.pmax(maxima, 'tgt')  11.3 us
    reduce_sum x2, other arithmetic, body(): totals = jnp.sum(jnp.exp(scores - maxima[:, None]), axis=1)  9.01 us
  transfers between devices with their start and end apart: 1, of which 1 were waited for; matrix products, arithmetic and copies ran while one was open for 1% of the time, Pallas kernels for 0%

commit v1 on v0

--- a/solution.py
+++ b/solution.py
@@ -26,7 +26,14 @@
     group_norm = jnp.sum(group_rows * group_rows, axis=1)
     cost_tile = cost_of(sources, src_norm, group_rows, group_norm)
     for repeat in range(ITERS):
-        group_pots = lax.all_gather(target_pots, "blk", axis=0, tiled=True)
+        ring = [target_pots]
+        for hop in range(7):
+            ring.append(lax.ppermute(ring[-1], "blk", [(dev, (dev + 1) % 8) for dev in range(8)]))
+        group_pots = jnp.roll(
+            jnp.concatenate(ring[::-1], axis=0),
+            (lax.axis_index("blk") + 1) * ring[0].shape[0],
+            axis=0,
+        )
         scores = (group_pots[None, :] - cost_tile) / EPS
         maxima = jnp.max(scores, axis=1)
         totals = jnp.sum(jnp.exp(scores - maxima[:, None]), axis=1)

time: 221 us -> 248 us (1.12)
  waiting for transfers between devices: 20.2 us -> 83.1 us
  blocking collectives: 139 us -> 97.8 us
  starting transfers between devices: 0.04 us -> 3.86 us
    ppermute x0 -> x14, waiting for transfers between devices: none -> 82.4 us  [body(): lax.ppermute(ring[-1], 'blk', [(dev, (dev + 1) % 8) for dev in range(8)])]
    all_gather x2 -> x0, blocking collectives: 40.8 us -> none  [body(): group_pots = lax.all_gather(target_pots, 'blk', axis=0, tiled=True)]
    all_gather x1, waiting for transfers between devices: 19.5 us -> 0.01 us  [body(): group_rows = lax.all_gather(targets, 'blk', axis=0, tiled=True)]
    ppermute x0 -> x14, starting transfers between devices: none -> 3.82 us  [body(): lax.ppermute(ring[-1], 'blk', [(dev, (dev + 1) % 8) for dev in range(8)])]
  transfers between devices with their start and end apart: 1 -> 15, of which waited for: 1 -> 14; matrix products, arithmetic and copies ran while one was open for 1% -> 1% of each run, Pallas kernels for 0% -> 0%
where the time goes in v1:
time: 248 us
  blocking collectives  97.8 us (39%)
  waiting for transfers between devices  83.1 us (34%)
  other arithmetic  34.7 us (14%)
  between operations  14.9 us (6%)
  matrix products  11.5 us (5%)
  starting transfers between devices  3.86 us (2%)
    ppermute x14, waiting for transfers between devices, body(): lax.ppermute(ring[-1], 'blk', [(dev, (dev + 1) % 8) for dev in range(8)])  82.4 us
    unnamed x2, blocking collectives  38 us
    pmax x2, blocking collectives, body(): col_high = lax.pmax(jnp.max(col_scores, axis=0), 'blk')  35.5 us
    psum x2, blocking collectives, body(): totals = lax.psum(totals * jnp.exp(maxima - highest), 'tgt')  13 us
    dot_general x1, matrix products, cost_of(): jnp.dot(left, right.T, preferred_element_type=jnp.float32, precision=lax....  11.5 us
    pmax x2, blocking collectives, body(): highest = lax.pmax(maxima, 'tgt')  11.3 us
    reduce_sum x2, other arithmetic, body(): totals = jnp.sum(jnp.exp(scores - maxima[:, None]), axis=1)  9.01 us
    reduce_sum x2, other arithmetic, body(): col_part = jnp.sum(jnp.exp(col_scores - col_high[None, :]), axis=0)  9.01 us
  transfers between devices with their start and end apart: 15, of which 14 were waited for; matrix products, arithmetic and copies ran while one was open for 1% of the time, Pallas kernels for 0%

profile of v1, /device:TPU:0, one launch (start us, length us, event | category | flops | bytes accessed | tf_op | source)
XLA Modules:
  0.0 247.8 jit_solution(13663073381564210351)
XLA Ops:
  7.9 3.0 %collective-permute-start = (f32[256]{0:T(256)}, f32[256]{0:T(256)S(1)}, u32[]{:S(2)}, u32[]{:S(2)}) collective-permute-start(f32[256]{0:T(256)} %param.7), channel_id=1, source_target_pairs={{0,4},{4,8},{8,12},{12,16},{16,20},{20,24},{24,28},{28,0},{1,5},{5... | collective-permute-start | bytes 3080 | tf_op jit(solution)/shard_map/ppermute | solution.py:31
  10.9 4.8 %collective-permute-done = f32[256]{0:T(256)S(1)} collective-permute-done((f32[256]{0:T(256)}, f32[256]{0:T(256)S(1)}, u32[]{:S(2)}, u32[]{:S(2)}) %collective-permute-start) | collective-permute-done | bytes 1056 | tf_op jit(solution)/shard_map/ppermute | solution.py:31
  15.7 6.3 %collective-permute-done.1 = f32[256]{0:T(256)S(1)} collective-permute-done((f32[256]{0:T(256)S(1)}, f32[256]{0:T(256)S(1)}, u32[]{:S(2)}, u32[]{:S(2)}) %collective-permute-start.1) | collective-permute-done | bytes 1056 | tf_op jit(solution)/shard_map/ppermute | solution.py:31
  22.0 6.3 %collective-permute-done.2 = f32[256]{0:T(256)S(1)} collective-permute-done((f32[256]{0:T(256)S(1)}, f32[256]{0:T(256)S(1)}, u32[]{:S(2)}, u32[]{:S(2)}) %collective-permute-start.2) | collective-permute-done | bytes 1056 | tf_op jit(solution)/shard_map/ppermute | solution.py:31
  28.3 6.3 %collective-permute-done.3 = f32[256]{0:T(256)S(1)} collective-permute-done((f32[256]{0:T(256)S(1)}, f32[256]{0:T(256)S(1)}, u32[]{:S(2)}, u32[]{:S(2)}) %collective-permute-start.3) | collective-permute-done | bytes 1056 | tf_op jit(solution)/shard_map/ppermute | solution.py:31
  35.8 5.0 %collective-permute-done.4 = f32[256]{0:T(256)S(1)} collective-permute-done((f32[256]{0:T(256)S(1)}, f32[256]{0:T(256)S(1)}, u32[]{:S(2)}, u32[]{:S(2)}) %collective-permute-start.4) | collective-permute-done | bytes 1056 | tf_op jit(solution)/shard_map/ppermute | solution.py:31
  40.8 6.3 %collective-permute-done.5 = f32[256]{0:T(256)S(1)} collective-permute-done((f32[256]{0:T(256)S(1)}, f32[256]{0:T(256)S(1)}, u32[]{:S(2)}, u32[]{:S(2)}) %collective-permute-start.5) | collective-permute-done | bytes 1056 | tf_op jit(solution)/shard_map/ppermute | solution.py:31
  49.0 4.4 %collective-permute-done.6 = f32[256]{0:T(256)S(1)} collective-permute-done((f32[256]{0:T(256)S(1)}, f32[256]{0:T(256)S(1)}, u32[]{:S(2)}, u32[]{:S(2)}) %collective-permute-start.6) | collective-permute-done | bytes 1056 | tf_op jit(solution)/shard_map/ppermute | solution.py:31
  54.2 1.6 multiply_reduce_fusion
  55.8 11.5 %fusion = (f32[1024]{0:T(1024)S(1)}, f32[1024,2048]{1,0:T(8,128)}) fusion(f32[2048]{0:T(1024)S(1)} %fusion.5, f32[1024,128]{1,0:T(8,128)} %param.5, f32[2048,128]{1,0:T(8,128)} %all-gather.2.cloned.1.call-done, f32[2048]{0:T(1024)S(1)} %multiply_reduce_fusion, f32[1024]{0:T(1024)S(1)} %multiply_reduce_fusion.1), kind=kOutput, calls=%fused_computation.9 | convolution fusion | flops 3233807360 | bytes 9986048 | tf_op jit(solution)/shard_map/dot_general | solution.py:11
  67.3 5.6 %pmax.28 = f32[1024]{0:T(1024)S(1)} all-reduce(f32[1024]{0:T(1024)S(1)} %get-tuple-element.3), channel_id=1, replica_groups=mesh['blk'=8,'tgt'=4] {'tgt'}, use_global_device_ids=true, to_apply=%region_3.5 | all-reduce | flops 1024 | bytes 8192 | tf_op jit(solution)/shard_map/pmax | solution.py:40
  72.9 4.5 %exponential_reduce_fusion.3 = f32[1024]{0:T(1024)S(1)} fusion(f32[1024,2048]{1,0:T(8,128)} %get-tuple-element.4, f32[1024]{0:T(1024)S(1)} %get-tuple-element.3, f32[2048]{0:T(1024)S(1)} %fusion.5), kind=kLoop, calls=%fused_computation.6 | loop fusion | flops 8387584 | bytes 8404992 | tf_op jit(solution)/shard_map/reduce_sum | solution.py:39
  77.5 6.8 %psum.14 = f32[1024]{0:T(1024)S(1)} all-reduce(f32[1024]{0:T(1024)S(1)} %exponential_multiply_fusion.1), channel_id=1, replica_groups=mesh['blk'=8,'tgt'=4] {'tgt'}, use_global_device_ids=true, to_apply=%region_5.7 | all-reduce | flops 1024 | bytes 8192 | tf_op jit(solution)/shard_map/psum | solution.py:41
  84.3 4.3 %fusion.1 = f32[2048]{0:T(1024)S(1)} fusion(f32[1024,2048]{1,0:T(8,128)} %get-tuple-element.4, f32[1024]{0:T(1024)S(1)} %multiply_subtract_fusion.2), kind=kLoop, calls=%fused_computation.10 | loop fusion | flops 6289408 | bytes 8400896 | tf_op jit(solution)/shard_map/reduce_max | solution.py:45
  88.6 18.1 %pmax.29 = f32[2048]{0:T(1024)S(1)} all-reduce(f32[2048]{0:T(1024)S(1)} %fusion.1), channel_id=1, replica_groups=mesh['blk'=8,'tgt'=4] {'blk'}, use_global_device_ids=true, to_apply=%region_7.9 | all-reduce | flops 2048 | bytes 16384 | tf_op jit(solution)/shard_map/pmax | solution.py:45
  106.7 4.5 %exponential_reduce_fusion.2 = f32[2048]{0:T(1024)S(1)} fusion(f32[1024,2048]{1,0:T(8,128)} %get-tuple-element.4, f32[2048]{0:T(1024)S(1)} %pmax.29, f32[1024]{0:T(1024)S(1)} %multiply_subtract_fusion.2), kind=kLoop, calls=%fused_computation.4 | loop fusion | flops 8386560 | bytes 8409088 | tf_op jit(solution)/shard_map/reduce_sum | solution.py:46
  111.3 18.6 %all-reduce = f32[2048]{0:T(1024)S(1)} all-reduce(f32[2048]{0:T(1024)S(1)} %exponential_reduce_fusion.2), channel_id=2, replica_groups=mesh['blk'=8,'tgt'=4] {'blk'}, use_global_device_ids=true, to_apply=%region_9.11.clone | all-reduce | flops 2048 | bytes 16384
  130.7 5.5 %collective-permute-done.7 = f32[256]{0:T(256)S(1)} collective-permute-done((f32[256]{0:T(256)S(1)}, f32[256]{0:T(256)S(1)}, u32[]{:S(2)}, u32[]{:S(2)}) %collective-permute-start.7) | collective-permute-done | bytes 1056 | tf_op jit(solution)/shard_map/ppermute | solution.py:31
  136.3 6.3 %collective-permute-done.8 = f32[256]{0:T(256)S(1)} collective-permute-done((f32[256]{0:T(256)S(1)}, f32[256]{0:T(256)S(1)}, u32[]{:S(2)}, u32[]{:S(2)}) %collective-permute-start.8) | collective-permute-done | bytes 1056 | tf_op jit(solution)/shard_map/ppermute | solution.py:31
  142.5 6.3 %collective-permute-done.9 = f32[256]{0:T(256)S(1)} collective-permute-done((f32[256]{0:T(256)S(1)}, f32[256]{0:T(256)S(1)}, u32[]{:S(2)}, u32[]{:S(2)}) %collective-permute-start.9) | collective-permute-done | bytes 1056 | tf_op jit(solution)/shard_map/ppermute | solution.py:31
  148.8 6.3 %collective-permute-done.10 = f32[256]{0:T(256)S(1)} collective-permute-done((f32[256]{0:T(256)S(1)}, f32[256]{0:T(256)S(1)}, u32[]{:S(2)}, u32[]{:S(2)}) %collective-permute-start.10) | collective-permute-done | bytes 1056 | tf_op jit(solution)/shard_map/ppermute | solution.py:31
  155.1 6.3 %collective-permute-done.11 = f32[256]{0:T(256)S(1)} collective-permute-done((f32[256]{0:T(256)S(1)}, f32[256]{0:T(256)S(1)}, u32[]{:S(2)}, u32[]{:S(2)}) %collective-permute-start.11) | collective-permute-done | bytes 1056 | tf_op jit(solution)/shard_map/ppermute | solution.py:31
  161.3 6.3 %collective-permute-done.12 = f32[256]{0:T(256)S(1)} collective-permute-done((f32[256]{0:T(256)S(1)}, f32[256]{0:T(256)S(1)}, u32[]{:S(2)}, u32[]{:S(2)}) %collective-permute-start.12) | collective-permute-done | bytes 1056 | tf_op jit(solution)/shard_map/ppermute | solution.py:31
  167.6 6.3 %collective-permute-done.13 = f32[256]{0:T(256)S(1)} collective-permute-done((f32[256]{0:T(256)S(1)}, f32[256]{0:T(256)S(1)}, u32[]{:S(2)}, u32[]{:S(2)}) %collective-permute-start.13) | collective-permute-done | bytes 1056 | tf_op jit(solution)/shard_map/ppermute | solution.py:31
  174.1 4.3 %fusion.2 = f32[1024]{0:T(1024)S(1)} fusion(f32[1024,2048]{1,0:T(8,128)} %get-tuple-element.4, f32[2048]{0:T(1024)S(1)} %fusion.4), kind=kLoop, calls=%fused_computation.11 | loop fusion | flops 6290432 | bytes 8400896 | tf_op jit(solution)/shard_map/reduce_max | solution.py:38
  178.4 4.5 %exponential_reduce_fusion.1 = f32[1024]{0:T(1024)S(1)} fusion(f32[1024,2048]{1,0:T(8,128)} %get-tuple-element.4, f32[1024]{0:T(1024)S(1)} %fusion.2, f32[2048]{0:T(1024)S(1)} %fusion.4), kind=kLoop, calls=%fused_computation.2 | loop fusion | flops 8387584 | bytes 8404992 | tf_op jit(solution)/shard_map/reduce_sum | solution.py:39
  182.9 5.7 %pmax.30 = f32[1024]{0:T(1024)S(1)} all-reduce(f32[1024]{0:T(1024)S(1)} %fusion.2), channel_id=1, replica_groups=mesh['blk'=8,'tgt'=4] {'tgt'}, use_global_device_ids=true, to_apply=%region_11.13 | all-reduce | flops 1024 | bytes 8192 | tf_op jit(solution)/shard_map/pmax | solution.py:40
  188.6 6.1 %psum.15 = f32[1024]{0:T(1024)S(1)} all-reduce(f32[1024]{0:T(1024)S(1)} %exponential_multiply_fusion), channel_id=1, replica_groups=mesh['blk'=8,'tgt'=4] {'tgt'}, use_global_device_ids=true, to_apply=%region_13.15 | all-reduce | flops 1024 | bytes 8192 | tf_op jit(solution)/shard_map/psum | solution.py:41
  194.7 4.3 %fusion.3 = f32[2048]{0:T(1024)S(1)} fusion(f32[1024,2048]{1,0:T(8,128)} %get-tuple-element.4, f32[1024]{0:T(1024)S(1)} %multiply_subtract_fusion.1), kind=kLoop, calls=%fused_computation.12 | loop fusion | flops 6289408 | bytes 8400896 | tf_op jit(solution)/shard_map/reduce_max | solution.py:45
  199.0 17.4 %pmax.31 = f32[2048]{0:T(1024)S(1)} all-reduce(f32[2048]{0:T(1024)S(1)} %fusion.3), channel_id=1, replica_groups=mesh['blk'=8,'tgt'=4] {'blk'}, use_global_device_ids=true, to_apply=%region_15.17 | all-reduce | flops 2048 | bytes 16384 | tf_op jit(solution)/shard_map/pmax | solution.py:45
  216.4 4.5 %exponential_reduce_fusion = f32[2048]{0:T(1024)S(1)} fusion(f32[1024,2048]{1,0:T(8,128)} %get-tuple-element.4, f32[2048]{0:T(1024)S(1)} %pmax.31, f32[1024]{0:T(1024)S(1)} %multiply_subtract_fusion.1), kind=kLoop, calls=%fused_computation | loop fusion | flops 8386560 | bytes 8409088 | tf_op jit(solution)/shard_map/reduce_sum | solution.py:46
  220.9 19.4 %all-reduce.1 = f32[2048]{0:T(1024)S(1)} all-reduce(f32[2048]{0:T(1024)S(1)} %exponential_reduce_fusion), channel_id=3, replica_groups=mesh['blk'=8,'tgt'=4] {'blk'}, use_global_device_ids=true, to_apply=%region_17.19.clone | all-reduce | flops 2048 | bytes 16384
  (46 shorter events, 5.7 us)
Async XLA Ops:
  7.2 47.1 %all-gather.2.cloned.1.call-start = ((), (), s32[]{:S(2)}) async-start(), calls=%async_computation | async-start | bytes 1179648 | tf_op jit(solution)/shard_map/all_gather | solution.py:25
  7.9 7.8 %collective-permute-start = (f32[256]{0:T(256)}, f32[256]{0:T(256)S(1)}, u32[]{:S(2)}, u32[]{:S(2)}) collective-permute-start(f32[256]{0:T(256)} %param.7), channel_id=1, source_target_pairs={{0,4},{4,8},{8,12},{12,16},{16,20},{20,24},{24,28},{28,0},{1,5},{5... | collective-permute-start | bytes 3080 | tf_op jit(solution)/shard_map/ppermute | solution.py:31
  15.7 6.3 %collective-permute-start.1 = (f32[256]{0:T(256)S(1)}, f32[256]{0:T(256)S(1)}, u32[]{:S(2)}, u32[]{:S(2)}) collective-permute-start(f32[256]{0:T(256)S(1)} %collective-permute-done), channel_id=1, source_target_pairs={{0,4},{4,8},{8,12},{12,16},{16,20},{20,24},{24,28},{28,0},{1,5},{5... | collective-permute-start | bytes 3080 | tf_op jit(solution)/shard_map/ppermute | solution.py:31
  22.0 6.3 %collective-permute-start.2 = (f32[256]{0:T(256)S(1)}, f32[256]{0:T(256)S(1)}, u32[]{:S(2)}, u32[]{:S(2)}) collective-permute-start(f32[256]{0:T(256)S(1)} %collective-permute-done.1), channel_id=1, source_target_pairs={{0,4},{4,8},{8,12},{12,16},{16,20},{20,24},{24,28},{28,0},{1,5},{5... | collective-permute-start | bytes 3080 | tf_op jit(solution)/shard_map/ppermute | solution.py:31
  28.3 6.3 %collective-permute-start.3 = (f32[256]{0:T(256)S(1)}, f32[256]{0:T(256)S(1)}, u32[]{:S(2)}, u32[]{:S(2)}) collective-permute-start(f32[256]{0:T(256)S(1)} %collective-permute-done.2), channel_id=1, source_target_pairs={{0,4},{4,8},{8,12},{12,16},{16,20},{20,24},{24,28},{28,0},{1,5},{5... | collective-permute-start | bytes 3080 | tf_op jit(solution)/shard_map/ppermute | solution.py:31
  34.5 6.3 %collective-permute-start.4 = (f32[256]{0:T(256)S(1)}, f32[256]{0:T(256)S(1)}, u32[]{:S(2)}, u32[]{:S(2)}) collective-permute-start(f32[256]{0:T(256)S(1)} %collective-permute-done.3), channel_id=1, source_target_pairs={{0,4},{4,8},{8,12},{12,16},{16,20},{20,24},{24,28},{28,0},{1,5},{5... | collective-permute-start | bytes 3080 | tf_op jit(solution)/shard_map/ppermute | solution.py:31
  40.8 6.3 %collective-permute-start.5 = (f32[256]{0:T(256)S(1)}, f32[256]{0:T(256)S(1)}, u32[]{:S(2)}, u32[]{:S(2)}) collective-permute-start(f32[256]{0:T(256)S(1)} %collective-permute-done.4), channel_id=1, source_target_pairs={{0,4},{4,8},{8,12},{12,16},{16,20},{20,24},{24,28},{28,0},{1,5},{5... | collective-permute-start | bytes 3080 | tf_op jit(solution)/shard_map/ppermute | solution.py:31
  47.1 6.3 %collective-permute-start.6 = (f32[256]{0:T(256)S(1)}, f32[256]{0:T(256)S(1)}, u32[]{:S(2)}, u32[]{:S(2)}) collective-permute-start(f32[256]{0:T(256)S(1)} %collective-permute-done.5), channel_id=1, source_target_pairs={{0,4},{4,8},{8,12},{12,16},{16,20},{20,24},{24,28},{28,0},{1,5},{5... | collective-permute-start | bytes 3080 | tf_op jit(solution)/shard_map/ppermute | solution.py:31
  130.0 6.3 %collective-permute-start.7 = (f32[256]{0:T(256)S(1)}, f32[256]{0:T(256)S(1)}, u32[]{:S(2)}, u32[]{:S(2)}) collective-permute-start(f32[256]{0:T(256)S(1)} %fusion.11), channel_id=1, source_target_pairs={{0,4},{4,8},{8,12},{12,16},{16,20},{20,24},{24,28},{28,0},{1,5},{5... | collective-permute-start | bytes 3080 | tf_op jit(solution)/shard_map/ppermute | solution.py:31
  136.3 6.3 %collective-permute-start.8 = (f32[256]{0:T(256)S(1)}, f32[256]{0:T(256)S(1)}, u32[]{:S(2)}, u32[]{:S(2)}) collective-permute-start(f32[256]{0:T(256)S(1)} %collective-permute-done.7), channel_id=1, source_target_pairs={{0,4},{4,8},{8,12},{12,16},{16,20},{20,24},{24,28},{28,0},{1,5},{5... | collective-permute-start | bytes 3080 | tf_op jit(solution)/shard_map/ppermute | solution.py:31
  142.5 6.3 %collective-permute-start.9 = (f32[256]{0:T(256)S(1)}, f32[256]{0:T(256)S(1)}, u32[]{:S(2)}, u32[]{:S(2)}) collective-permute-start(f32[256]{0:T(256)S(1)} %collective-permute-done.8), channel_id=1, source_target_pairs={{0,4},{4,8},{8,12},{12,16},{16,20},{20,24},{24,28},{28,0},{1,5},{5... | collective-permute-start | bytes 3080 | tf_op jit(solution)/shard_map/ppermute | solution.py:31
  148.8 6.3 %collective-permute-start.10 = (f32[256]{0:T(256)S(1)}, f32[256]{0:T(256)S(1)}, u32[]{:S(2)}, u32[]{:S(2)}) collective-permute-start(f32[256]{0:T(256)S(1)} %collective-permute-done.9), channel_id=1, source_target_pairs={{0,4},{4,8},{8,12},{12,16},{16,20},{20,24},{24,28},{28,0},{1,5},{5... | collective-permute-start | bytes 3080 | tf_op jit(solution)/shard_map/ppermute | solution.py:31
  155.1 6.3 %collective-permute-start.11 = (f32[256]{0:T(256)S(1)}, f32[256]{0:T(256)S(1)}, u32[]{:S(2)}, u32[]{:S(2)}) collective-permute-start(f32[256]{0:T(256)S(1)} %collective-permute-done.10), channel_id=1, source_target_pairs={{0,4},{4,8},{8,12},{12,16},{16,20},{20,24},{24,28},{28,0},{1,5},{5... | collective-permute-start | bytes 3080 | tf_op jit(solution)/shard_map/ppermute | solution.py:31
  161.3 6.3 %collective-permute-start.12 = (f32[256]{0:T(256)S(1)}, f32[256]{0:T(256)S(1)}, u32[]{:S(2)}, u32[]{:S(2)}) collective-permute-start(f32[256]{0:T(256)S(1)} %collective-permute-done.11), channel_id=1, source_target_pairs={{0,4},{4,8},{8,12},{12,16},{16,20},{20,24},{24,28},{28,0},{1,5},{5... | collective-permute-start | bytes 3080 | tf_op jit(solution)/shard_map/ppermute | solution.py:31
  167.6 6.3 %collective-permute-start.13 = (f32[256]{0:T(256)S(1)}, f32[256]{0:T(256)S(1)}, u32[]{:S(2)}, u32[]{:S(2)}) collective-permute-start(f32[256]{0:T(256)S(1)} %collective-permute-done.12), channel_id=1, source_target_pairs={{0,4},{4,8},{8,12},{12,16},{16,20},{20,24},{24,28},{28,0},{1,5},{5... | collective-permute-start | bytes 3080 | tf_op jit(solution)/shard_map/ppermute | solution.py:31
  194.7 26.2 %copy-start = (f32[1024]{0:T(1024)}, f32[1024]{0:T(1024)S(1)}, u32[]{:S(2)}) copy-start(f32[1024]{0:T(1024)S(1)} %multiply_subtract_fusion.1) | copy-start | bytes 12292
Sparse Core Ops, SparseCore 0:
  10.1 43.0 all-gather.1
